TPU v7x, 8 devices: a whole 2x2x1 slice. The times are simulated.
8 devices in a mesh: fsdp: 8 (over z, y, x, core).
Axes of the slice: x: 2, y: 2, z: 1, core: 2. Of those that a mesh axis runs over, the one named last changes fastest.
Arguments:
- hidden: bfloat16 [64, 512, 1536], P('fsdp')
- grad_out: bfloat16 [64, 512, 1536], P('fsdp')
- positions: int32 [64, 512], P('fsdp')
- gain_attn: bfloat16 [1536], P('fsdp')
- w_q: bfloat16 [1536, 1536], P('fsdp')
- b_q: bfloat16 [1536], P('fsdp')
- w_k: bfloat16 [1536, 256], P('fsdp')
- b_k: bfloat16 [256], P('fsdp')
- w_v: bfloat16 [1536, 256], P('fsdp')
- b_v: bfloat16 [256], P('fsdp')
- w_o: bfloat16 [1536, 1536], P('fsdp')
- gain_mlp: bfloat16 [1536], P('fsdp')
- w_gate: bfloat16 [1536, 8960], P('fsdp')
- w_up: bfloat16 [1536, 8960], P('fsdp')
- w_down: bfloat16 [8960, 1536], P('fsdp')
Outputs:
- output 1: bfloat16 [64, 512, 1536], P('fsdp')
- output 2: bfloat16 [64, 512, 1536], P('fsdp')
- output 3: float32 [1536], P('fsdp')
- output 4: float32 [1536, 1536], P('fsdp')
- output 5: float32 [1536], P('fsdp')
- output 6: float32 [1536, 256], P('fsdp')
- output 7: float32 [256], P('fsdp')
- output 8: float32 [1536, 256], P('fsdp')
- output 9: float32 [256], P('fsdp')
- output 10: float32 [1536, 1536], P('fsdp')
- output 11: float32 [1536], P('fsdp')
- output 12: float32 [1536, 8960], P('fsdp')
- output 13: float32 [1536, 8960], P('fsdp')
- output 14: float32 [8960, 1536], P('fsdp')
All inputs are finite; a program needn't handle non-finite values.
Results may differ from a plain program's by a relative error of at most 0.0163765.
Values are sent between devices in bfloat16 or wider.
A program may use at most 1 GiB of HBM per device.

v0:
```python
import math
import jax
import jax.numpy as jnp
from jax import lax
from jax.sharding import PartitionSpec as P

HEAD_DIM = 128
NORM_EPS = 1e-6
ROPE_THETA = 1000000.0
FSDP_AXIS = 'fsdp'


def matmul_f32(eq_form, lhs_arr, rhs_arr):
    return jnp.einsum(eq_form, lhs_arr, rhs_arr, preferred_element_type=jnp.float32)


def rope_tables(positions):
    inv_freq = 1.0 / jnp.power(ROPE_THETA, jnp.arange(0, HEAD_DIM, 2).astype(jnp.float32) / HEAD_DIM)
    angles = positions.astype(jnp.float32)[:, :, None] * inv_freq
    angles = jnp.concatenate([angles, angles], axis=-1)[:, :, None, :]
    return jnp.cos(angles), jnp.sin(angles)


def rotate_half(vec_in):
    half_dim = vec_in.shape[-1] // 2
    return jnp.concatenate([-vec_in[..., half_dim:], vec_in[..., :half_dim]], axis=-1)


def rotate_half_t(vec_in):
    half_dim = vec_in.shape[-1] // 2
    return jnp.concatenate([vec_in[..., half_dim:], -vec_in[..., :half_dim]], axis=-1)


def norm_fwd(hidden, gain_vec):
    x_f32 = hidden.astype(jnp.float32)
    inv_rms = lax.rsqrt(jnp.mean(x_f32 * x_f32, axis=-1, keepdims=True) + NORM_EPS)
    return (x_f32 * inv_rms * gain_vec.astype(jnp.float32)).astype(jnp.bfloat16), inv_rms


def norm_bwd(hidden, inv_rms, gain_vec, d_normed):
    unit_rows = hidden.astype(jnp.float32) * inv_rms
    d_gain = jnp.sum(d_normed * unit_rows, axis=(0, 1))
    d_unit = d_normed * gain_vec.astype(jnp.float32)
    d_hidden = inv_rms * (d_unit - unit_rows * jnp.mean(d_unit * unit_rows, axis=-1, keepdims=True))
    return d_hidden, d_gain


def layer_fwd(hidden, positions, weights):
    gain_attn, w_q, b_q, w_k, b_k, w_v, b_v, w_o, gain_mlp, w_gate, w_up, w_down = weights
    n_batch = hidden.shape[0]
    n_seq = hidden.shape[1]
    n_heads = w_q.shape[1] // HEAD_DIM
    n_kv = w_k.shape[1] // HEAD_DIM
    q_per_kv = n_heads // n_kv
    cos_t, sin_t = rope_tables(positions)
    normed_attn, inv_attn = norm_fwd(hidden, gain_attn)
    q_lin = (matmul_f32('bsd,de->bse', normed_attn, w_q) + b_q.astype(jnp.float32)).reshape(n_batch, n_seq, n_heads, HEAD_DIM)
    k_lin = (matmul_f32('bsd,de->bse', normed_attn, w_k) + b_k.astype(jnp.float32)).reshape(n_batch, n_seq, n_kv, HEAD_DIM)
    v_states = (matmul_f32('bsd,de->bse', normed_attn, w_v) + b_v.astype(jnp.float32)).astype(jnp.bfloat16)
    v_states = v_states.reshape(n_batch, n_seq, n_kv, HEAD_DIM)
    q_states = (q_lin * cos_t + rotate_half(q_lin) * sin_t).astype(jnp.bfloat16)
    q_states = q_states.reshape(n_batch, n_seq, n_kv, q_per_kv, HEAD_DIM)
    k_states = (k_lin * cos_t + rotate_half(k_lin) * sin_t).astype(jnp.bfloat16)
    scores = matmul_f32('bqkgd,bskd->bkgqs', q_states, k_states) / math.sqrt(HEAD_DIM)
    causal = lax.broadcasted_iota(jnp.int32, (n_seq, n_seq), 0) >= lax.broadcasted_iota(jnp.int32, (n_seq, n_seq), 1)
    attn_probs = jax.nn.softmax(jnp.where(causal, scores, -1e30), axis=-1)
    attn_out = matmul_f32('bkgqs,bskd->bqkgd', attn_probs.astype(jnp.bfloat16), v_states).astype(jnp.bfloat16)
    attn_out = attn_out.reshape(n_batch, n_seq, n_heads * HEAD_DIM)
    resid_mid = (hidden.astype(jnp.float32) + matmul_f32('bse,ed->bsd', attn_out, w_o)).astype(jnp.bfloat16)
    normed_mlp, inv_mlp = norm_fwd(resid_mid, gain_mlp)
    gate_pre = matmul_f32('bsd,df->bsf', normed_mlp, w_gate)
    up_proj = matmul_f32('bsd,df->bsf', normed_mlp, w_up)
    act_mlp = (jax.nn.silu(gate_pre) * up_proj).astype(jnp.bfloat16)
    layer_out = (resid_mid.astype(jnp.float32) + matmul_f32('bsf,fd->bsd', act_mlp, w_down)).astype(jnp.bfloat16)
    saved_acts = {'cos_t': cos_t, 'sin_t': sin_t, 'normed_attn': normed_attn, 'inv_attn': inv_attn, 'q_states': q_states, 'k_states': k_states, 'v_states': v_states, 'attn_probs': attn_probs, 'attn_out': attn_out, 'resid_mid': resid_mid, 'normed_mlp': normed_mlp, 'inv_mlp': inv_mlp, 'gate_pre': gate_pre, 'up_proj': up_proj, 'act_mlp': act_mlp}
    return layer_out, saved_acts


def layer_bwd(hidden, grad_out, saved_acts, weights):
    gain_attn, w_q, b_q, w_k, b_k, w_v, b_v, w_o, gain_mlp, w_gate, w_up, w_down = weights
    n_batch = hidden.shape[0]
    n_seq = hidden.shape[1]
    n_heads = w_q.shape[1] // HEAD_DIM
    n_kv = w_k.shape[1] // HEAD_DIM
    q_per_kv = n_heads // n_kv
    cos_t = saved_acts['cos_t']
    sin_t = saved_acts['sin_t']
    d_w_down = matmul_f32('bsf,bsd->fd', saved_acts['act_mlp'], grad_out)
    d_act = matmul_f32('bsd,fd->bsf', grad_out, w_down).astype(jnp.bfloat16).astype(jnp.float32)
    gate_pre = saved_acts['gate_pre']
    gate_sig = jax.nn.sigmoid(gate_pre)
    d_gate = (d_act * saved_acts['up_proj'] * gate_sig * (1.0 + gate_pre * (1.0 - gate_sig))).astype(jnp.bfloat16)
    d_up = (d_act * gate_pre * gate_sig).astype(jnp.bfloat16)
    normed_mlp = saved_acts['normed_mlp']
    d_w_gate = matmul_f32('bsd,bsf->df', normed_mlp, d_gate)
    d_w_up = matmul_f32('bsd,bsf->df', normed_mlp, d_up)
    d_normed_mlp = (matmul_f32('bsf,df->bsd', d_gate, w_gate) + matmul_f32('bsf,df->bsd', d_up, w_up)).astype(jnp.bfloat16).astype(jnp.float32)
    d_resid_norm, d_gain_mlp = norm_bwd(saved_acts['resid_mid'], saved_acts['inv_mlp'], gain_mlp, d_normed_mlp)
    d_resid = (grad_out.astype(jnp.float32) + d_resid_norm).astype(jnp.bfloat16)
    d_w_o = matmul_f32('bse,bsd->ed', saved_acts['attn_out'], d_resid)
    d_attn = matmul_f32('bsd,ed->bse', d_resid, w_o).astype(jnp.bfloat16).reshape(n_batch, n_seq, n_kv, q_per_kv, HEAD_DIM)
    attn_probs = saved_acts['attn_probs']
    d_v_states = matmul_f32('bkgqs,bqkgd->bskd', attn_probs.astype(jnp.bfloat16), d_attn).astype(jnp.bfloat16)
    d_probs = matmul_f32('bqkgd,bskd->bkgqs', d_attn, saved_acts['v_states'])
    d_scores = (attn_probs * (d_probs - jnp.sum(attn_probs * d_probs, axis=-1, keepdims=True)) / math.sqrt(HEAD_DIM)).astype(jnp.bfloat16)
    d_q_rot = matmul_f32('bkgqs,bskd->bqkgd', d_scores, saved_acts['k_states']).astype(jnp.bfloat16).astype(jnp.float32)
    d_q_rot = d_q_rot.reshape(n_batch, n_seq, n_heads, HEAD_DIM)
    d_k_rot = matmul_f32('bkgqs,bqkgd->bskd', d_scores, saved_acts['q_states']).astype(jnp.bfloat16).astype(jnp.float32)
    d_q_lin = (d_q_rot * cos_t + rotate_half_t(d_q_rot * sin_t)).reshape(n_batch, n_seq, n_heads * HEAD_DIM)
    d_k_lin = (d_k_rot * cos_t + rotate_half_t(d_k_rot * sin_t)).reshape(n_batch, n_seq, n_kv * HEAD_DIM)
    d_v_lin = d_v_states.reshape(n_batch, n_seq, n_kv * HEAD_DIM)
    d_b_q = jnp.sum(d_q_lin, axis=(0, 1))
    d_b_k = jnp.sum(d_k_lin, axis=(0, 1))
    d_b_v = jnp.sum(d_v_lin.astype(jnp.float32), axis=(0, 1))
    d_q_bf = d_q_lin.astype(jnp.bfloat16)
    d_k_bf = d_k_lin.astype(jnp.bfloat16)
    normed_attn = saved_acts['normed_attn']
    d_w_q = matmul_f32('bsd,bse->de', normed_attn, d_q_bf)
    d_w_k = matmul_f32('bsd,bse->de', normed_attn, d_k_bf)
    d_w_v = matmul_f32('bsd,bse->de', normed_attn, d_v_lin)
    d_normed_attn = (matmul_f32('bse,de->bsd', d_q_bf, w_q) + matmul_f32('bse,de->bsd', d_k_bf, w_k) + matmul_f32('bse,de->bsd', d_v_lin, w_v)).astype(jnp.bfloat16).astype(jnp.float32)
    d_hidden_norm, d_gain_attn = norm_bwd(hidden, saved_acts['inv_attn'], gain_attn, d_normed_attn)
    grad_hidden = (d_resid.astype(jnp.float32) + d_hidden_norm).astype(jnp.bfloat16)
    grad_list = (d_gain_attn, d_w_q, d_b_q, d_w_k, d_b_k, d_w_v, d_b_v, d_w_o, d_gain_mlp, d_w_gate, d_w_up, d_w_down)
    return grad_hidden, grad_list


def gather_all(shards):
    return tuple(lax.all_gather(w_shard, FSDP_AXIS, axis=0, tiled=True) for w_shard in shards)


def solution(mesh):
    act_spec = P(FSDP_AXIS, None, None)
    mat_spec = P(FSDP_AXIS, None)
    vec_spec = P(FSDP_AXIS)
    param_specs = (vec_spec, mat_spec, vec_spec, mat_spec, vec_spec, mat_spec, vec_spec, mat_spec, vec_spec, mat_spec, mat_spec, mat_spec)
    in_specs_all = (act_spec, act_spec, mat_spec) + param_specs
    out_specs_all = (act_spec, act_spec) + param_specs

    def local_step(hidden, grad_out, positions, *shards):
        full_fwd = gather_all(shards)
        layer_out, saved_acts = layer_fwd(hidden, positions, full_fwd)
        shards_bwd, saved_acts = lax.optimization_barrier((shards, saved_acts))
        full_bwd = gather_all(shards_bwd)
        grad_hidden, grad_list = layer_bwd(hidden, grad_out, saved_acts, full_bwd)
        grad_shards = tuple(lax.psum_scatter(grad_part, FSDP_AXIS, scatter_dimension=0, tiled=True) for grad_part in grad_list)
        return (layer_out, grad_hidden) + grad_shards

    return jax.shard_map(local_step, mesh=mesh, in_specs=in_specs_all, out_specs=out_specs_all, check_vma=False)
```

profile of v0, /device:TPU:0, one launch (start us, length us, event | category | flops | bytes accessed | tf_op | source)
XLA Modules:
  0.0 2943.2 jit_solution(3687664459639586443)
XLA Ops:
  14.4 26.2 all-reduce.14
  142.8 28.3 convolution_add_fusion
  171.1 24.8 copy.81
  231.2 51.4 %fusion.111 = (f32[8,2,6,512]{3,2,1,0:T(8,128)S(1)}, f32[8,2,6,512,512]{3,4,2,1,0:T(8,128)}) fusion(pred[512,512]{0,1:T(8,128)(4,1)S(1)} %iota_compare_fusion, bf16[8,512,2,6,128]{1,4,3,2,0:T(8,128)(2,1)} %fusion.57, bf16[8,512,2,128]{1,3,2,0:T(8,128)(2,1)} %fusion.76), kind=kOutput, calls=%fused_computation.159 | convolution fusion | flops 6543114752 | bytes 115802112 | tf_op jit(solution)/shard_map/sub | solution.py:66
  282.6 65.8 %broadcast_divide_fusion = f32[8,2,6,512,512]{3,4,2,1,0:T(8,128)} fusion(f32[8,2,6,512,512]{3,4,2,1,0:T(8,128)} %get-tuple-element.101, f32[8,2,6,512]{3,2,1,0:T(8,128)S(1)} %get-tuple-element.100), kind=kLoop, calls=%fused_computation.24 | loop fusion | flops 25165824 | bytes 201523200 | tf_op jit(solution)/shard_map/div | solution.py:66
  348.5 37.7 %fusion.67 = bf16[8,2,128,6,512]{4,2,3,1,0:T(8,128)(2,1)} fusion(bf16[8,512,2,128,1]{1,3,4,2,0:T(8,128)(2,1)S(1)} %bitcast.275, f32[8,2,6,512,512]{3,4,2,1,0:T(8,128)} %broadcast_divide_fusion), kind=kOutput, calls=%fused_computation.101 | convolution fusion | flops 6473908224 | bytes 115343360 | tf_op jit(solution)/shard_map/bkgqs,bskd->bqkgd/dot_general | solution.py:14
  386.1 30.6 %fusion.48 = (f32[8,512]{1,0:T(8,128)S(1)}, bf16[8,512,1536]{2,1,0:T(8,128)(2,1)}) fusion(bf16[8,512,1536]{1,2,0:T(8,128)(2,1)} %bitcast.270, bf16[1536,1536]{1,0:T(8,128)(2,1)} %all-gather.13.cloned.1.call-done, bf16[8,512,1536]{2,1,0:T(8,128)(2,1)} %param.15), kind=kOutput, calls=%fused_computation.71 | convolution fusion | flops 19365097472 | bytes 42483712 | tf_op jit(solution)/shard_map/bse,ed->bsd/dot_general | solution.py:14
  429.0 126.3 %fusion.36 = f32[8,512,8960]{2,1,0:T(8,128)} fusion(bf16[8,512,1536]{2,1,0:T(8,128)(2,1)} %fusion.50, bf16[1536,8960]{1,0:T(8,128)(2,1)} %all-gather.15.cloned.1.call-done), kind=kOutput, calls=%fused_computation.59 | convolution fusion | flops 112742891520 | bytes 186908672 | tf_op jit(solution)/shard_map/bsd,df->bsf/dot_general | solution.py:14
  555.3 155.5 %multiply_convert_fusion = (bf16[8,512,8960]{2,1,0:T(8,128)(2,1)}, f32[8,512,8960]{2,1,0:T(8,128)}) fusion(f32[8,512,8960]{2,1,0:T(8,128)} %fusion.36, bf16[8,512,1536]{2,1,0:T(8,128)(2,1)} %fusion.50, bf16[1536,8960]{1,0:T(8,128)(2,1)} %all-gather.17.cloned.1.call-done), kind=kOutput, calls=%fused_computation.10 | convolution fusion | flops 112963092480 | bytes 407109632 | tf_op jit(solution)/shard_map/bsd,df->bsf/dot_general | solution.py:14
  714.3 23.6 all-reduce.13
  738.6 103.5 %all-gather.21.cloned.1.call-done = bf16[8960,1536]{1,0:T(8,128)(2,1)} async-done(((bf16[1120,1536]{1,0:T(8,128)(2,1)}), bf16[8960,1536]{1,0:T(8,128)(2,1)}) %all-gather.21.cloned.1.call-update) | async-done | bytes 27525136 | tf_op jit(solution)/shard_map/all_gather | solution.py:129
  842.1 204.4 %fusion.4 = (bf16[8,512,8960]{2,1,0:T(8,128)(2,1)}, bf16[8,512,8960]{2,1,0:T(8,128)(2,1)}) fusion(f32[8,512,8960]{2,1,0:T(8,128)} %get-tuple-element.40, f32[8,512,8960]{2,1,0:T(8,128)} %fusion.36, bf16[8,512,1536]{2,1,0:T(8,128)(2,1)} %param.16, bf16[8960,1536]{1,0:T(8,128)(2,1)} %all-gather.21.cloned.1.call-done), kind=kOutput, calls=%fused_computation.6 | convolution fusion | flops 113293393920 | bytes 480509952 | tf_op jit(solution)/shard_map/bsd,fd->bsf/dot_general | solution.py:14
  1046.5 126.9 %fusion.27 = f32[8,512,1536]{2,1,0:T(8,128)} fusion(bf16[8,512,8960]{2,1,0:T(8,128)(2,1)} %get-tuple-element.79, bf16[1536,8960]{1,0:T(8,128)(2,1)} %all-gather.25.cloned.1.call-done), kind=kOutput, calls=%fused_computation.50 | convolution fusion | flops 112742891520 | bytes 126091264 | tf_op jit(solution)/shard_map/bsf,df->bsd/dot_general | solution.py:14
  1173.4 137.6 %fusion.45 = (f32[1536]{0:T(1024)}, f32[8,512]{1,0:T(8,128)S(1)}, bf16[8,512,1536]{2,1,0:T(8,128)(2,1)}) fusion(bf16[8,512,1536]{2,1,0:T(8,128)(2,1)} %get-tuple-element.45, f32[8,512]{1,0:T(8,128)S(1)} %bitcast.280, f32[1536]{0:T(1024)S(1)} %copy-done.18, f32[8,512,1536]{2,1,0:T(8,128)} %fusion.27, bf16[8,512,8960]{2,1,0:T(8,128)(2,1)} %get-tuple-element.78, ...), kind=kOutput, calls=%fused_computation.68 | convolution fusion | flops 112805806080 | bytes 151302144 | tf_op jit(solution)/shard_map/bsf,df->bsd/dot_general | solution.py:14
  1330.4 25.4 convolution_convert_fusion.1
  1372.5 37.8 %convert_reduce_fusion = (f32[2,128]{1,0:T(2,128)}, bf16[8,2,128,512]{3,2,1,0:T(8,128)(2,1)S(1)}) fusion(bf16[8,512,2,6,128]{1,4,3,2,0:T(8,128)(2,1)} %bitcast.257, f32[8,2,6,512,512]{3,4,2,1,0:T(8,128)} %broadcast_divide_fusion), kind=kOutput, calls=%fused_computation.115 | convolution fusion | flops 6470762496 | bytes 115344384 | tf_op jit(solution)/shard_map/bkgqs,bqkgd->bskd/dot_general | solution.py:14
  1418.7 39.4 %fusion.83 = f32[8,2,512,512,6]{3,2,4,1,0:T(8,128)} fusion(bf16[8,512,2,6,128]{1,4,3,2,0:T(8,128)(2,1)} %bitcast.258, bf16[8,512,2,128]{1,3,2,0:T(8,128)(2,1)} %bitcast.274), kind=kOutput, calls=%fused_computation.127 | convolution fusion | flops 6442450944 | bytes 115343360 | tf_op jit(solution)/shard_map/bqkgd,bskd->bkgqs/dot_general | solution.py:14
  1458.2 126.8 %bitcast_multiply_fusion.14 = (f32[8,512,2,128]{1,3,2,0:T(8,128)}, bf16[8,2,128,512]{3,2,1,0:T(8,128)(2,1)}) fusion(f32[8,512,128]{1,2,0:T(8,128)} %bitcast.276, bf16[8,512,2,6,128]{1,4,3,2,0:T(8,128)(2,1)} %fusion.57, f32[8,2,6,512,512]{3,4,2,1,0:T(8,128)} %broadcast_divide_fusion, f32[8,2,512,512,6]{3,2,4,1,0:T(8,128)} %fusion.83), kind=kOutput, calls=%fused_computation.112 | convolution fusion | flops 6571475456 | bytes 222298112 | tf_op jit(solution)/shard_map/bkgqs,bqkgd->bskd/dot_general | solution.py:14
  1599.9 28.1 convolution_bitcast_fusion.3
  1628.0 137.2 %convert_convert_fusion = f32[8,2,128,6,512]{4,2,3,1,0:T(8,128)} fusion(f32[8,2,6,512,512]{3,4,2,1,0:T(8,128)} %broadcast_divide_fusion, f32[8,2,512,512,6]{3,2,4,1,0:T(8,128)} %fusion.83, bf16[8,512,2,128]{1,3,2,0:T(8,128)(2,1)} %fusion.76), kind=kOutput, calls=%fused_computation.97 | convolution fusion | flops 6580912640 | bytes 228589568 | tf_op jit(solution)/shard_map/bkgqs,bskd->bqkgd/dot_general | solution.py:14
  1783.7 20.7 fusion.109
  1841.4 28.0 convolution_bitcast_fusion.4
  1869.5 129.9 %convolution_bitcast_fusion.2 = f32[8960,1536]{1,0:T(8,128)} fusion(bf16[8,512,8960]{2,1,0:T(8,128)(2,1)} %get-tuple-element.61, bf16[8,512,1536]{2,1,0:T(8,128)(2,1)} %param.16), kind=kOutput, calls=%fused_computation.37 | convolution fusion | flops 112742891520 | bytes 141033472 | tf_op jit(solution)/shard_map/bsf,bsd->fd/dot_general | solution.py:14
  1999.5 131.1 %convolution_bitcast_fusion = f32[1536,8960]{1,0:T(8,128)} fusion(bf16[8,512,1536]{2,1,0:T(8,128)(2,1)} %fusion.50, bf16[8,512,8960]{2,1,0:T(8,128)(2,1)} %get-tuple-element.79), kind=kOutput, calls=%fused_computation.35 | convolution fusion | flops 112742891520 | bytes 141033472 | tf_op jit(solution)/shard_map/bsd,bsf->df/dot_general | solution.py:14
  2130.7 129.7 %convolution_bitcast_fusion.1 = f32[1536,8960]{1,0:T(8,128)} fusion(bf16[8,512,1536]{2,1,0:T(8,128)(2,1)} %fusion.50, bf16[8,512,8960]{2,1,0:T(8,128)(2,1)} %get-tuple-element.78), kind=kOutput, calls=%fused_computation.36 | convolution fusion | flops 112742891520 | bytes 141033472 | tf_op jit(solution)/shard_map/bsd,bsf->df/dot_general | solution.py:14
  2261.7 22.1 all_gather.81
  2303.5 130.3 %fusion.51 = bf16[8,512,1536]{2,1,0:T(8,128)(2,1)} fusion(bf16[8,512,1536]{2,1,0:T(8,128)(2,1)} %get-tuple-element.45, bf16[8,512,8960]{2,1,0:T(8,128)(2,1)} %get-tuple-element.61, bf16[8960,1536]{1,0:T(8,128)(2,1)} %all-gather.19.cloned.1.call-done), kind=kOutput, calls=%fused_computation.74 | convolution fusion | flops 112761765888 | bytes 126091264 | tf_op jit(solution)/shard_map/bsf,fd->bsd/dot_general | solution.py:14
  2464.4 27.2 fusion.70
  2491.7 29.1 fusion.47
  2520.8 23.9 all-reduce.12
  2568.4 58.3 %reduce-scatter.18.cloned.1.call-done = f32[192,8960]{1,0:T(8,128)} async-done(((f32[1536,8960]{1,0:T(8,128)}), f32[192,8960]{1,0:T(8,128)}) %reduce-scatter.18.cloned.1.call-update) | async-done | bytes 6881296 | tf_op jit(solution)/shard_map/reduce_scatter | solution.py:146
  2626.7 309.5 %reduce-scatter.16.cloned.1.call-done = f32[192,8960]{1,0:T(8,128)} async-done(((f32[1536,8960]{1,0:T(8,128)}), f32[192,8960]{1,0:T(8,128)}) %reduce-scatter.16.cloned.1.call-update) | async-done | bytes 6881296 | tf_op jit(solution)/shard_map/reduce_scatter | solution.py:146
  (174 shorter events, 351.0 us)
Async XLA Ops:
  7.2 41.3 %copy-start.19 = (s32[8,512]{1,0:T(8,128)S(1)}, s32[8,512]{1,0:T(8,128)}, u32[]{:S(2)}) copy-start(s32[8,512]{1,0:T(8,128)} %param.17) | copy-start | bytes 49156
  7.2 135.6 %all-gather.11.cloned.1.call-start = ((), (), s32[]{:S(2)}) async-start(), calls=%async_computation.7 | async-start | bytes 5308416 | tf_op jit(solution)/shard_map/all_gather | solution.py:129
  7.9 378.2 %all-gather.13.cloned.1.call-start = ((), (), s32[]{:S(2)}) async-start(), calls=%async_computation.8 | async-start | bytes 5308416 | tf_op jit(solution)/shard_map/all_gather | solution.py:129
  8.7 420.4 %all-gather.15.cloned.1.call-start = ((), (), s32[]{:S(2)}) async-start(), calls=%async_computation.9 | async-start | bytes 30965760 | tf_op jit(solution)/shard_map/all_gather | solution.py:129
  9.4 46.7 %copy-start.11 = (bf16[192,256]{1,0:T(8,128)(2,1)S(1)}, bf16[192,256]{1,0:T(8,128)(2,1)}, u32[]{:S(2)}) copy-start(bf16[192,256]{1,0:T(8,128)(2,1)} %param.21) | copy-start | bytes 294916
  9.4 545.9 %all-gather.17.cloned.1.call-start = ((), (), s32[]{:S(2)}) async-start(), calls=%async_computation.10 | async-start | bytes 30965760 | tf_op jit(solution)/shard_map/all_gather | solution.py:129
  10.0 832.1 %all-gather.21.cloned.1.call-start = ((), (), s32[]{:S(2)}) async-start(), calls=%async_computation.12 | async-start | bytes 30965760 | tf_op jit(solution)/shard_map/all_gather | solution.py:129
  56.0 81.4 %copy-start.2 = (f32[8,512,128]{1,2,0:T(8,128)}, f32[8,512,128]{1,2,0:T(8,128)S(1)}, u32[]{:S(2)}) copy-start(f32[8,512,128]{1,2,0:T(8,128)S(1)} %get-tuple-element.93) | copy-start | bytes 6291460
  282.6 65.8 %copy-start.7 = (bf16[8,512,256]{1,2,0:T(8,128)(2,1)S(1)}, bf16[8,512,256]{1,2,0:T(8,128)(2,1)}, u32[]{:S(2)}) copy-start(bf16[8,512,256]{1,2,0:T(8,128)(2,1)} %add_convert_fusion.2) | copy-start | bytes 6291460
  386.1 31.2 %copy-start.17 = (f32[1536]{0:T(1024)S(1)}, f32[1536]{0:T(1024)}, u32[]{:S(2)}) copy-start(f32[1536]{0:T(1024)} %convert_element_type.181) | copy-start | bytes 18436
  710.9 335.6 %all-gather.25.cloned.1.call-start = ((), (), s32[]{:S(2)}) async-start(), calls=%async_computation.14 | async-start | bytes 30965760 | tf_op jit(solution)/shard_map/all_gather | solution.py:129
  711.5 461.9 %all-gather.23.cloned.1.call-start = ((), (), s32[]{:S(2)}) async-start(), calls=%async_computation.13 | async-start | bytes 30965760 | tf_op jit(solution)/shard_map/all_gather | solution.py:129
  712.2 618.2 %all-gather.27.cloned.1.call-start = ((), (), s32[]{:S(2)}) async-start(), calls=%async_computation.15 | async-start | bytes 5308416 | tf_op jit(solution)/shard_map/all_gather | solution.py:129
  713.0 1590.6 %all-gather.19.cloned.1.call-start = ((), (), s32[]{:S(2)}) async-start(), calls=%async_computation.11 | async-start | bytes 30965760 | tf_op jit(solution)/shard_map/all_gather | solution.py:129
  713.7 1750.7 %all-gather.29.cloned.1.call-start = ((), (), s32[]{:S(2)}) async-start(), calls=%async_computation.16 | async-start | bytes 5308416 | tf_op jit(solution)/shard_map/all_gather | solution.py:129
  738.5 1829.9 %reduce-scatter.12.cloned.1.call-start = ((), (), s32[]{:S(2)}) async-start(), calls=%async_computation.19 | async-start | bytes 1769472 | tf_op jit(solution)/shard_map/reduce_scatter | solution.py:146
  1046.5 126.9 %copy-start.16 = (f32[8,512,1]{1,0,2:T(8,128)S(1)}, f32[8,512,1]{1,0,2:T(8,128)}, u32[]{:S(2)}) copy-start(f32[8,512,1]{1,0,2:T(8,128)} %get-tuple-element.38) | copy-start | bytes 49156
  1046.5 126.9 %copy-start.18 = (f32[1536]{0:T(1024)S(1)}, f32[1536]{0:T(1024)}, u32[]{:S(2)}) copy-start(f32[1536]{0:T(1024)} %convert_element_type.193) | copy-start | bytes 18436
  1410.3 47.8 %copy-start.5 = (bf16[8,2,128,512]{3,2,1,0:T(8,128)(2,1)}, bf16[8,2,128,512]{3,2,1,0:T(8,128)(2,1)S(1)}, u32[]{:S(2)}) copy-start(bf16[8,2,128,512]{3,2,1,0:T(8,128)(2,1)S(1)} %get-tuple-element.111) | copy-start | bytes 6291460
  1458.1 1110.3 %reduce-scatter.10.cloned.1.call-start = ((), (), s32[]{:S(2)}) async-start(), calls=%async_computation.18 | async-start | bytes 1769472 | tf_op jit(solution)/shard_map/reduce_scatter | solution.py:146
  1458.2 129.7 %copy-start = (f32[8,512,1,128]{1,3,0,2:T(8,128)S(1)}, f32[8,512,1,128]{1,3,0,2:T(8,128)}, u32[]{:S(2)}) copy-start(f32[8,512,1,128]{1,3,0,2:T(8,128)} %get-tuple-element.51) | copy-start | bytes 6291460
  1599.8 968.6 %reduce-scatter.14.cloned.1.call-start = ((), (), s32[]{:S(2)}) async-start(), calls=%async_computation.20 | async-start | bytes 10616832 | tf_op jit(solution)/shard_map/reduce_scatter | solution.py:146
  1627.9 940.5 %reduce-scatter.8.cloned.1.call-start = ((), (), s32[]{:S(2)}) async-start(), calls=%async_computation.17 | async-start | bytes 10616832 | tf_op jit(solution)/shard_map/reduce_scatter | solution.py:146
  1783.7 41.1 %slice-start = ((s8[25165824]{0:T(1024)(128)(4,1)}), s8[4194304]{0:T(1024)(128)(4,1)S(1)}, s32[]{:S(2)}) async-start(s8[25165824]{0:T(1024)(128)(4,1)} %bitcast.255), calls=%async_computation.24 | async-start | bytes 8388608
  1783.7 41.1 %slice-start.1 = ((s8[25165824]{0:T(1024)(128)(4,1)}), s8[4194304]{0:T(1024)(128)(4,1)S(1)}, s32[]{:S(2)}) async-start(s8[25165824]{0:T(1024)(128)(4,1)} %bitcast.255), calls=%async_computation.25 | async-start | bytes 8388608
  1783.7 41.1 %slice-start.2 = ((s8[25165824]{0:T(1024)(128)(4,1)}), s8[4194304]{0:T(1024)(128)(4,1)S(1)}, s32[]{:S(2)}) async-start(s8[25165824]{0:T(1024)(128)(4,1)} %bitcast.255), calls=%async_computation.26 | async-start | bytes 8388608
  1869.4 699.0 %reduce-scatter.20.cloned.1.call-start = ((), (), s32[]{:S(2)}) async-start(), calls=%async_computation.23 | async-start | bytes 61931520 | tf_op jit(solution)/shard_map/reduce_scatter | solution.py:146
  1999.4 627.3 %reduce-scatter.18.cloned.1.call-start = ((), (), s32[]{:S(2)}) async-start(), calls=%async_computation.22 | async-start | bytes 61931520 | tf_op jit(solution)/shard_map/reduce_scatter | solution.py:146
  2130.6 805.6 %reduce-scatter.16.cloned.1.call-start = ((), (), s32[]{:S(2)}) async-start(), calls=%async_computation.21 | async-start | bytes 61931520 | tf_op jit(solution)/shard_map/reduce_scatter | solution.py:146
  2303.5 130.4 %copy-start.1 = (f32[8,512,1,128]{1,3,0,2:T(8,128)S(1)}, f32[8,512,1,128]{1,3,0,2:T(8,128)}, u32[]{:S(2)}) copy-start(f32[8,512,1,128]{1,3,0,2:T(8,128)} %get-tuple-element.51) | copy-start | bytes 6291460
  2491.6 29.2 copy-start.20
  2491.7 29.2 copy-start.22
  (17 other events, 274.3 us)
Sparse Core Ops, SparseCore 0:
  9.8 37.1 all-gather.10
  48.8 35.9 all-gather.12
  86.6 134.5 all-gather.14
  222.8 129.5 all-gather.16
  711.0 131.0 all-gather.20
  843.7 129.5 all-gather.24
  975.2 129.5 all-gather.22
  1106.6 33.2 all-gather.26
  1141.7 129.6 all-gather.18
  1273.0 33.2 all-gather.28
  1458.2 30.6 reduce-scatter.11
  1599.9 30.6 reduce-scatter.9
  1634.6 68.4 reduce-scatter.13
  1869.6 69.2 reduce-scatter.7
  1999.5 316.1 reduce-scatter.19
  2319.7 306.9 reduce-scatter.17
  2630.7 305.4 reduce-scatter.15
where the time goes:
time: 2950 us; the launch traced here: 2940 us
  matrix products  1950 us (66%)
  waiting for transfers between devices  477 us (16%)
  other arithmetic  299 us (10%)
  blocking collectives  153 us (5%)
  local copies, waits for them, and re-layouts  51.4 us (2%)
    dot_general x26, matrix products, matmul_f32(): jnp.einsum(eq_form, lhs_arr, rhs_arr, preferred_element_type=jnp.float32)  1900 us
    reduce_scatter x7, waiting for transfers between devices, local_step(): lax.psum_scatter(grad_part, FSDP_AXIS, scatter_dimension=0, tiled=True)  368 us
    all_gather x10, waiting for transfers between devices, gather_all(): lax.all_gather(w_shard, FSDP_AXIS, axis=0, tiled=True)  104 us
    all_gather x4, blocking collectives, gather_all(): lax.all_gather(w_shard, FSDP_AXIS, axis=0, tiled=True)  79.4 us
    unnamed x3, blocking collectives  73.7 us
    div x1, other arithmetic, layer_fwd(): attn_probs = jax.nn.softmax(jnp.where(causal, scores, -1e+30), axis=-1)  65.8 us
  transfers between devices with their start and end apart: 17, of which 3 were waited for; matrix products, arithmetic and copies ran while one was open for 73% of the time, Pallas kernels for 0%

commit v1 on v0

v1 whole, which is shorter than its diff:
```python
import functools
import math
import jax
import jax.numpy as jnp
from jax import lax
from jax.experimental import pallas as pl
from jax.experimental.pallas import tpu as pltpu
from jax.sharding import PartitionSpec as P

HEAD_DIM = 128
NORM_EPS = 1e-6
ROPE_THETA = 1000000.0
FSDP_AXIS = 'fsdp'
LOG2E = 1.4426950408889634
Q_BLK = 256
NT = (((1,), (1,)), ((), ()))
NN = (((1,), (0,)), ((), ()))


def matmul_f32(eq_form, lhs_arr, rhs_arr):
    return jnp.einsum(eq_form, lhs_arr, rhs_arr, preferred_element_type=jnp.float32)


def dot_f32(lhs_arr, rhs_arr, dims):
    return lax.dot_general(lhs_arr, rhs_arr, dims, preferred_element_type=jnp.float32)


def rope_tables(positions):
    inv_freq = 1.0 / jnp.power(ROPE_THETA, jnp.arange(0, HEAD_DIM, 2).astype(jnp.float32) / HEAD_DIM)
    angles = positions.astype(jnp.float32).reshape(-1, 1) * inv_freq
    cos_h, sin_h = jnp.cos(angles), jnp.sin(angles)
    return jnp.concatenate([cos_h, cos_h], axis=-1), jnp.concatenate([-sin_h, sin_h], axis=-1)


def causal_keep(n_blk):
    key_i = lax.broadcasted_iota(jnp.int32, (n_blk, n_blk), 0)
    qry_i = lax.broadcasted_iota(jnp.int32, (n_blk, n_blk), 1)
    return key_i <= qry_i


def attn_fwd_kernel(n_group, q_ref, k_ref, v_ref, cos_ref, sin_ref, o_ref, qr_ref, kr_ref, vb_ref, lse_ref):
    n_seq = k_ref.shape[0]
    cos_t, sin_t = cos_ref[...], sin_ref[...]
    score_mul = LOG2E / math.sqrt(HEAD_DIM)
    keep = causal_keep(Q_BLK)

    def rope(vec_in):
        return (vec_in * cos_t + pltpu.roll(vec_in, HEAD_DIM // 2, 1) * sin_t).astype(jnp.bfloat16)

    kr_ref[...] = rope(k_ref[...])
    v_f32 = v_ref[...].astype(jnp.bfloat16).astype(jnp.float32)
    vb_ref[...] = v_f32.astype(jnp.bfloat16)
    v_tr = v_f32.T.astype(jnp.bfloat16)
    for h in range(n_group):
        cols = pl.ds(h * HEAD_DIM, HEAD_DIM)
        qr_ref[:, cols] = rope(q_ref[:, cols])
    for h in range(n_group):
        cols = pl.ds(h * HEAD_DIM, HEAD_DIM)
        for blk in range(n_seq // Q_BLK):
            rows = pl.ds(blk * Q_BLK, Q_BLK)
            n_key = (blk + 1) * Q_BLK
            scores = dot_f32(kr_ref[0:n_key, :], qr_ref[rows, cols], NT)
            diag = jnp.where(keep, scores[n_key - Q_BLK:, :], -1e30)
            if blk:
                scores = jnp.concatenate([scores[:n_key - Q_BLK, :], diag], axis=0)
            else:
                scores = diag
            row_max = jnp.max(scores, axis=0, keepdims=True)
            exp_s = jnp.exp2((scores - row_max) * score_mul)
            row_sum = jnp.sum(exp_s, axis=0, keepdims=True)
            probs = (exp_s * (1.0 / row_sum)).astype(jnp.bfloat16)
            o_tr = dot_f32(v_tr[:, :n_key], probs, NN)
            o_ref[rows, cols] = o_tr.T.astype(jnp.bfloat16)
            lse_ref[0, h:h + 1, rows] = row_max * score_mul + jnp.log2(row_sum)


def attn_bwd_kernel(n_group, n_q, n_kv_w, q_ref, k_ref, v_ref, do_ref, lse_ref, cos_ref, sin_ref, d_ref, db_ref, dk_acc, dv_acc):
    n_seq = k_ref.shape[0]
    kv_i = pl.program_id(1)
    cos_t, sin_t = cos_ref[...], sin_ref[...]
    scale = 1.0 / math.sqrt(HEAD_DIM)
    score_mul = LOG2E * scale
    keep = causal_keep(Q_BLK)
    k_tr = k_ref[...].astype(jnp.float32).T.astype(jnp.bfloat16)

    def rope_t(vec_in, rows):
        d_rot = vec_in.astype(jnp.bfloat16).astype(jnp.float32)
        return d_rot * cos_t[rows] - pltpu.roll(d_rot, HEAD_DIM // 2, 1) * sin_t[rows]

    for h in range(n_group):
        cols = pl.ds(h * HEAD_DIM, HEAD_DIM)
        out_cols = pl.ds(pl.multiple_of((kv_i * n_group + h) * HEAD_DIM, HEAD_DIM), HEAD_DIM)
        bias_sum = jnp.zeros((1, HEAD_DIM), jnp.float32)
        for blk in range(n_seq // Q_BLK):
            rows = pl.ds(blk * Q_BLK, Q_BLK)
            n_key = (blk + 1) * Q_BLK
            q_blk, do_blk = q_ref[rows, cols], do_ref[rows, cols]
            scores = dot_f32(k_ref[0:n_key, :], q_blk, NT)
            probs = jnp.exp2(scores * score_mul - lse_ref[0, h:h + 1, rows])
            diag = jnp.where(keep, probs[n_key - Q_BLK:, :], 0.0)
            if blk:
                probs = jnp.concatenate([probs[:n_key - Q_BLK, :], diag], axis=0)
            else:
                probs = diag
            d_probs = dot_f32(v_ref[0:n_key, :], do_blk, NT)
            delta = jnp.sum(probs * d_probs, axis=0, keepdims=True)
            d_scores = (probs * (d_probs - delta) * scale).astype(jnp.bfloat16)
            dv_part = dot_f32(probs.astype(jnp.bfloat16), do_blk, NN)
            dk_part = dot_f32(d_scores, q_blk, NN)
            if h == 0:
                tail = pl.ds(n_key - Q_BLK, Q_BLK)
                if blk:
                    dv_acc[0:n_key - Q_BLK, :] += dv_part[:n_key - Q_BLK, :]
                    dk_acc[0:n_key - Q_BLK, :] += dk_part[:n_key - Q_BLK, :]
                dv_acc[tail, :] = dv_part[n_key - Q_BLK:, :]
                dk_acc[tail, :] = dk_part[n_key - Q_BLK:, :]
            else:
                dv_acc[0:n_key, :] += dv_part
                dk_acc[0:n_key, :] += dk_part
            dq_blk = dot_f32(k_tr[:, :n_key], d_scores, NN).T
            dq_lin = rope_t(dq_blk, slice(blk * Q_BLK, (blk + 1) * Q_BLK))
            bias_sum = bias_sum + jnp.sum(dq_lin, axis=0, keepdims=True)
            d_ref[rows, out_cols] = dq_lin.astype(jnp.bfloat16)
        db_ref[0, :, out_cols] = bias_sum
    dk_lin = rope_t(dk_acc[...], slice(0, n_seq))
    dv_lin = dv_acc[...].astype(jnp.bfloat16)
    k_cols = pl.ds(pl.multiple_of(n_q + kv_i * HEAD_DIM, HEAD_DIM), HEAD_DIM)
    v_cols = pl.ds(pl.multiple_of(n_q + n_kv_w + kv_i * HEAD_DIM, HEAD_DIM), HEAD_DIM)
    d_ref[:, k_cols] = dk_lin.astype(jnp.bfloat16)
    d_ref[:, v_cols] = dv_lin
    db_ref[0, :, k_cols] = jnp.sum(dk_lin, axis=0, keepdims=True)
    db_ref[0, :, v_cols] = jnp.sum(dv_lin.astype(jnp.float32), axis=0, keepdims=True)


def attention_fwd(qkv_lin, cos_t, sin_t, n_batch, n_seq, n_q, n_kv):
    n_tok = n_batch * n_seq
    n_group = n_q // HEAD_DIM // n_kv
    grp_w = n_group * HEAD_DIM
    q_heads = n_q // HEAD_DIM
    flops = 4 * n_tok * n_seq * n_q * 3 // 4
    return pl.pallas_call(
        functools.partial(attn_fwd_kernel, n_group),
        grid=(n_batch, n_kv),
        in_specs=[
            pl.BlockSpec((n_seq, grp_w), lambda b, j: (b, j)),
            pl.BlockSpec((n_seq, HEAD_DIM), lambda b, j: (b, q_heads + j)),
            pl.BlockSpec((n_seq, HEAD_DIM), lambda b, j: (b, q_heads + n_kv + j)),
            pl.BlockSpec((n_seq, HEAD_DIM), lambda b, j: (b, 0)),
            pl.BlockSpec((n_seq, HEAD_DIM), lambda b, j: (b, 0)),
        ],
        out_specs=[
            pl.BlockSpec((n_seq, grp_w), lambda b, j: (b, j)),
            pl.BlockSpec((n_seq, grp_w), lambda b, j: (b, j)),
            pl.BlockSpec((n_seq, HEAD_DIM), lambda b, j: (b, j)),
            pl.BlockSpec((n_seq, HEAD_DIM), lambda b, j: (b, j)),
            pl.BlockSpec((1, 8, n_seq), lambda b, j: (b * n_kv + j, 0, 0)),
        ],
        out_shape=[
            jax.ShapeDtypeStruct((n_tok, n_q), jnp.bfloat16),
            jax.ShapeDtypeStruct((n_tok, n_q), jnp.bfloat16),
            jax.ShapeDtypeStruct((n_tok, n_kv * HEAD_DIM), jnp.bfloat16),
            jax.ShapeDtypeStruct((n_tok, n_kv * HEAD_DIM), jnp.bfloat16),
            jax.ShapeDtypeStruct((n_batch * n_kv, 8, n_seq), jnp.float32),
        ],
        compiler_params=pltpu.CompilerParams(dimension_semantics=('arbitrary', 'arbitrary'), vmem_limit_bytes=48 * 2**20),
        cost_estimate=pl.CostEstimate(flops=flops * 3, bytes_accessed=n_tok * n_q * 10, transcendentals=n_tok * n_seq * q_heads),
        name='attn_fwd',
    )(qkv_lin, qkv_lin, qkv_lin, cos_t, sin_t)


def attention_bwd(q_rot, k_rot, v_bf, d_attn, lse, cos_t, sin_t, n_batch, n_seq, n_kv):
    n_tok, n_q = q_rot.shape
    n_group = n_q // HEAD_DIM // n_kv
    grp_w = n_group * HEAD_DIM
    n_kv_w = n_kv * HEAD_DIM
    n_all = n_q + 2 * n_kv_w
    flops = 10 * n_tok * n_seq * n_q * 3 // 4
    return pl.pallas_call(
        functools.partial(attn_bwd_kernel, n_group, n_q, n_kv_w),
        grid=(n_batch, n_kv),
        in_specs=[
            pl.BlockSpec((n_seq, grp_w), lambda b, j: (b, j)),
            pl.BlockSpec((n_seq, HEAD_DIM), lambda b, j: (b, j)),
            pl.BlockSpec((n_seq, HEAD_DIM), lambda b, j: (b, j)),
            pl.BlockSpec((n_seq, grp_w), lambda b, j: (b, j)),
            pl.BlockSpec((1, 8, n_seq), lambda b, j: (b * n_kv + j, 0, 0)),
            pl.BlockSpec((n_seq, HEAD_DIM), lambda b, j: (b, 0)),
            pl.BlockSpec((n_seq, HEAD_DIM), lambda b, j: (b, 0)),
        ],
        out_specs=[
            pl.BlockSpec((n_seq, n_all), lambda b, j: (b, 0)),
            pl.BlockSpec((1, 1, n_all), lambda b, j: (b, 0, 0)),
        ],
        out_shape=[
            jax.ShapeDtypeStruct((n_tok, n_all), jnp.bfloat16),
            jax.ShapeDtypeStruct((n_batch, 1, n_all), jnp.float32),
        ],
        scratch_shapes=[pltpu.VMEM((n_seq, HEAD_DIM), jnp.float32), pltpu.VMEM((n_seq, HEAD_DIM), jnp.float32)],
        compiler_params=pltpu.CompilerParams(dimension_semantics=('arbitrary', 'arbitrary'), vmem_limit_bytes=48 * 2**20),
        cost_estimate=pl.CostEstimate(flops=flops * 3, bytes_accessed=n_tok * n_q * 8, transcendentals=n_tok * n_seq * n_q // HEAD_DIM),
        name='attn_bwd',
    )(q_rot, k_rot, v_bf, d_attn, lse, cos_t, sin_t)


def inv_rms_of(hidden):
    x_f32 = hidden.astype(jnp.float32)
    return lax.rsqrt(jnp.mean(x_f32 * x_f32, axis=-1, keepdims=True) + NORM_EPS)


def norm_apply(hidden, inv_rms, gain_vec):
    return (hidden.astype(jnp.float32) * inv_rms * gain_vec.astype(jnp.float32)).astype(jnp.bfloat16)


def norm_bwd(hidden, inv_rms, gain_vec, d_normed):
    unit_rows = hidden.astype(jnp.float32) * inv_rms
    d_gain = jnp.sum(d_normed * unit_rows, axis=0)
    d_unit = d_normed * gain_vec.astype(jnp.float32)
    d_hidden = inv_rms * (d_unit - unit_rows * jnp.mean(d_unit * unit_rows, axis=-1, keepdims=True))
    return d_hidden, d_gain


def gather_rows(shard):
    return lax.all_gather(shard, FSDP_AXIS, axis=0, tiled=True)


def scatter_rows(grad_part):
    return lax.psum_scatter(grad_part, FSDP_AXIS, scatter_dimension=0, tiled=True)


def after(value, *earlier):
    return lax.optimization_barrier((value,) + earlier)[0]


def solution(mesh):
    act_spec = P(FSDP_AXIS, None, None)
    mat_spec = P(FSDP_AXIS, None)
    vec_spec = P(FSDP_AXIS)
    param_specs = (vec_spec, mat_spec, vec_spec, mat_spec, vec_spec, mat_spec, vec_spec, mat_spec, vec_spec, mat_spec, mat_spec, mat_spec)
    in_specs_all = (act_spec, act_spec, mat_spec) + param_specs
    out_specs_all = (act_spec, act_spec) + param_specs
    n_dev = mesh.shape[FSDP_AXIS]

    def local_step(hidden3, grad_out3, positions, *shards):
        s_gain_attn, s_wq, s_bq, s_wk, s_bk, s_wv, s_bv, s_wo, s_gain_mlp, s_gate, s_up, s_down = shards
        n_batch, n_seq, n_model = hidden3.shape
        n_tok = n_batch * n_seq
        hidden = hidden3.reshape(n_tok, n_model)
        grad_out = grad_out3.reshape(n_tok, n_model)
        n_rows, n_q = s_wq.shape
        n_kv_w = s_wk.shape[1]
        n_kv = n_kv_w // HEAD_DIM
        n_all = n_q + 2 * n_kv_w

        def column(vec):
            return jnp.pad(vec, (0, n_rows - vec.shape[0]))[:, None]

        small = jnp.concatenate([column(s_gain_attn), column(s_gain_mlp), column(s_bq), column(s_bk), column(s_bv), jnp.zeros((n_rows, 123), jnp.bfloat16)], axis=1)
        packed = gather_rows(jnp.concatenate([s_wq, s_wk, s_wv, small], axis=1))
        w_qkv = packed[:, :n_all]
        vecs = packed[:, n_all:n_all + 5]
        gain_attn, gain_mlp, b_q = vecs[:, 0], vecs[:, 1], vecs[:, 2]
        kv_rows = vecs.reshape(n_dev, n_rows, 5)[:, :n_kv_w // n_dev, :]
        b_k, b_v = kv_rows[:, :, 3].reshape(n_kv_w), kv_rows[:, :, 4].reshape(n_kv_w)
        b_qkv = jnp.concatenate([b_q, b_k, b_v]).astype(jnp.float32)
        w_o = gather_rows(s_wo)
        w_gate, w_up, w_down = gather_rows(s_gate), gather_rows(s_up), gather_rows(s_down)

        cos_t, sin_t = rope_tables(positions)
        inv_attn = inv_rms_of(hidden)
        normed_attn = norm_apply(hidden, inv_attn, gain_attn)
        qkv_lin = matmul_f32('td,de->te', normed_attn, w_qkv) + b_qkv
        attn_out, q_rot, k_rot, v_bf, lse = attention_fwd(qkv_lin, cos_t, sin_t, n_batch, n_seq, n_q, n_kv)
        resid_mid = (hidden.astype(jnp.float32) + matmul_f32('te,ed->td', attn_out, w_o)).astype(jnp.bfloat16)
        inv_mlp = inv_rms_of(resid_mid)
        normed_mlp = norm_apply(resid_mid, inv_mlp, gain_mlp)
        gate_pre = matmul_f32('td,df->tf', normed_mlp, w_gate)
        up_proj = matmul_f32('td,df->tf', normed_mlp, w_up)
        act_mlp = (jax.nn.silu(gate_pre) * up_proj).astype(jnp.bfloat16)

        d_w_down = matmul_f32('tf,td->fd', act_mlp, grad_out)
        g_down = scatter_rows(d_w_down)
        grad_out_b = after(grad_out, d_w_down)
        d_act = matmul_f32('td,fd->tf', grad_out_b, w_down).astype(jnp.bfloat16).astype(jnp.float32)
        gate_sig = jax.nn.sigmoid(gate_pre)
        d_gate = (d_act * up_proj * gate_sig * (1.0 + gate_pre * (1.0 - gate_sig))).astype(jnp.bfloat16)
        d_up = (d_act * gate_pre * gate_sig).astype(jnp.bfloat16)
        d_w_gate = matmul_f32('td,tf->df', normed_mlp, d_gate)
        g_gate = scatter_rows(d_w_gate)
        d_w_up = matmul_f32('td,tf->df', after(normed_mlp, d_w_gate), d_up)
        g_up = scatter_rows(d_w_up)
        d_gate_b, d_up_b = lax.optimization_barrier((d_gate, d_up, d_w_up))[:2]
        d_normed_mlp = (matmul_f32('tf,df->td', d_gate_b, w_gate) + matmul_f32('tf,df->td', d_up_b, w_up)).astype(jnp.bfloat16).astype(jnp.float32)
        d_resid_norm, d_gain_mlp = norm_bwd(resid_mid, inv_mlp, gain_mlp, d_normed_mlp)
        d_resid = (grad_out.astype(jnp.float32) + d_resid_norm).astype(jnp.bfloat16)
        d_w_o = matmul_f32('te,td->ed', attn_out, d_resid)
        g_o = scatter_rows(d_w_o)
        d_attn = matmul_f32('td,ed->te', after(d_resid, d_w_o), w_o).astype(jnp.bfloat16)
        d_qkv, d_bias_rows = attention_bwd(q_rot, k_rot, v_bf, d_attn, lse, cos_t, sin_t, n_batch, n_seq, n_kv)
        d_w_qkv = matmul_f32('td,te->de', normed_attn, d_qkv)
        g_qkv = scatter_rows(d_w_qkv)
        d_qkv_b, act_last = lax.optimization_barrier((d_qkv, act_mlp, d_w_qkv))[:2]
        d_normed_attn = matmul_f32('te,de->td', d_qkv_b, w_qkv).astype(jnp.bfloat16).astype(jnp.float32)
        d_hidden_norm, d_gain_attn = norm_bwd(hidden, inv_attn, gain_attn, d_normed_attn)
        grad_hidden = (d_resid.astype(jnp.float32) + d_hidden_norm).astype(jnp.bfloat16)
        layer_out = (resid_mid.astype(jnp.float32) + matmul_f32('tf,fd->td', act_last, w_down)).astype(jnp.bfloat16)

        d_bias = jnp.sum(d_bias_rows, axis=(0, 1))
        g_gain_attn, g_gain_mlp = scatter_rows(d_gain_attn), scatter_rows(d_gain_mlp)
        g_bq = scatter_rows(d_bias[:n_q])
        g_bk, g_bv = scatter_rows(d_bias[n_q:n_q + n_kv_w]), scatter_rows(d_bias[n_q + n_kv_w:])
        g_wq, g_wk, g_wv = g_qkv[:, :n_q], g_qkv[:, n_q:n_q + n_kv_w], g_qkv[:, n_q + n_kv_w:]
        return (layer_out.reshape(hidden3.shape), grad_hidden.reshape(hidden3.shape), g_gain_attn, g_wq, g_bq, g_wk, g_bk, g_wv, g_bv, g_o, g_gain_mlp, g_gate, g_up, g_down)


    return jax.shard_map(local_step, mesh=mesh, in_specs=in_specs_all, out_specs=out_specs_all, check_vma=False)
```

time: 2950 us -> 2640 us (0.89)
  matrix products: 1950 us -> 1430 us
  waiting for transfers between devices: 477 us -> 911 us
  other arithmetic: 299 us -> 73.8 us
  Pallas kernels: 0 us -> 154 us
  blocking collectives: 153 us -> 23.6 us
    reduce_scatter x7 -> x5, waiting for transfers between devices: 368 us -> 864 us  [scatter_rows(): lax.psum_scatter(grad_part, FSDP_AXIS, scatter_dimension=0, tiled=True)]
    dot_general x26 -> x15, matrix products: 1900 us -> 1430 us  [matmul_f32(): jnp.einsum(eq_form, lhs_arr, rhs_arr, preferred_element_type=jnp.float32)]
    pallas_call x0 -> x2, Pallas kernels: none -> 154 us  [the longest x1 88.7 us: attention_bwd(): pl.pallas_call(functools.partial(attn_bwd_kernel, n_group, n_q, n_kv_w),...]
    all_gather x4 -> x0, blocking collectives: 79.4 us -> none  [gather_all(): lax.all_gather(w_shard, FSDP_AXIS, axis=0, tiled=True)]
    div x1 -> x0, other arithmetic: 65.8 us -> none  [layer_fwd(): attn_probs = jax.nn.softmax(jnp.where(causal, scores, -1e+30), axis=-1)]
    all_gather x10 -> x5, waiting for transfers between devices: 104 us -> 41.6 us  [gather_rows(): return lax.all_gather(shard, FSDP_AXIS, axis=0, tiled=True)]
    convert_element_type x15 -> x6, other arithmetic: 107 us -> 55.7 us  [the longest x2 19.9 us: norm_apply(): (hidden.astype(jnp.float32) * inv_rms * gain_vec.astype(jnp.float32)).ast...]
    sub x1 -> x0, matrix products: 51.4 us -> none  [layer_fwd(): attn_probs = jax.nn.softmax(jnp.where(causal, scores, -1e+30), axis=-1)]
  transfers between devices with their start and end apart: 17 -> 10, of which waited for: 3 -> 6; matrix products, arithmetic and copies ran while one was open for 73% -> 27% of each run, Pallas kernels for 0% -> 2%
where the time goes in v1:
time: 2640 us; the launch traced here: 2630 us
  matrix products  1430 us (54%)
  waiting for transfers between devices  911 us (35%)
  Pallas kernels  154 us (6%)
  other arithmetic  73.8 us (3%)
    dot_general x15, matrix products, matmul_f32(): jnp.einsum(eq_form, lhs_arr, rhs_arr, preferred_element_type=jnp.float32)  1430 us
    reduce_scatter x5, waiting for transfers between devices, scatter_rows(): lax.psum_scatter(grad_part, FSDP_AXIS, scatter_dimension=0, tiled=True)  864 us
    pallas_call x1, Pallas kernels, attention_bwd(): pl.pallas_call(functools.partial(attn_bwd_kernel, n_group, n_q, n_kv_w),...  88.7 us
    pallas_call x1, Pallas kernels, attention_fwd(): pl.pallas_call(functools.partial(attn_fwd_kernel, n_group), grid=(n_batch...  65.4 us
  transfers between devices with their start and end apart: 10, of which 6 were waited for; matrix products, arithmetic and copies ran while one was open for 27% of the time, Pallas kernels for 2%

profile of v1, /device:TPU:0, one launch (start us, length us, event | category | flops | bytes accessed | tf_op | source)
XLA Modules:
  0.0 2631.2 jit_solution(12452787825279222719)
XLA Ops:
  15.8 7.3 fusion.28
  23.2 7.5 fusion.32
  30.7 3.2 pad_maximum_fusion
  33.8 23.7 all-gather.6.cloned.1.call-done
  61.3 8.1 fusion.27
  69.8 32.1 %convolution_add_fusion.q_ref.k_ref.v_ref = f32[4096,2048]{1,0:T(8,128)} fusion(bf16[4096,1536]{1,0:T(8,128)(2,1)S(1)} %fusion.27, f32[2048]{0:T(1024)S(1)} %maximum_convert_fusion, bf16[1536,2176]{1,0:T(8,128)(2,1)S(1)} %bitcast.62), kind=kOutput, calls=%fused_computation.45 | convolution fusion | flops 25778192384 | bytes 52436992 | tf_op jit(solution)/shard_map/td,de->te/dot_general | solution.py:21
  101.9 65.4 %attn_fwd.1 = (bf16[4096,1536]{1,0:T(8,128)(2,1)}, bf16[4096,1536]{1,0:T(8,128)(2,1)}, bf16[4096,256]{1,0:T(8,128)(2,1)S(1)}, bf16[4096,256]{1,0:T(8,128)(2,1)S(1)}, f32[16,8,512]{2,1,0:T(8,128)S(1)}) custom-call(f32[4096,2048]{1,0:T(8,128)} %convolution_add_fusion.q_ref.k_ref.v_ref, f32[4096,2048]{1,0:T(8,128)} %convolution_add_fusion.q_ref.k_ref.v_ref, ...), custom_call_target="tpu_custom_call" | custom-call | flops 28991029248 | bytes 62914560 | tf_op jit(solution)/shard_map/attn_fwd/pallas_call | solution.py:141
  168.6 30.4 %fusion.23 = (f32[4096]{0:T(1024)S(1)}, bf16[4096,1536]{1,0:T(8,128)(2,1)}) fusion(bf16[4096,1536]{1,0:T(8,128)(2,1)} %get-tuple-element.28, bf16[1536,1536]{1,0:T(8,128)(2,1)} %all-gather.8.cloned.1.call-done, bf16[8,512,1536]{2,1,0:T(8,128)(2,1)} %param.15), kind=kOutput, calls=%fused_computation.34 | convolution fusion | flops 19365097472 | bytes 42483712 | tf_op jit(solution)/shard_map/te,ed->td/dot_general | solution.py:21
  199.6 11.8 fusion.20
  211.4 12.7 all-gather.10.cloned.1.call-done
  224.1 126.0 %fusion.35 = f32[4096,8960]{1,0:T(8,128)} fusion(bf16[4096,1536]{1,0:T(8,128)(2,1)} %fusion.20, bf16[1536,8960]{1,0:T(8,128)(2,1)} %all-gather.10.cloned.1.call-done), kind=kOutput, calls=%fused_computation.69 | convolution fusion | flops 112742891520 | bytes 186908672 | tf_op jit(solution)/shard_map/td,df->tf/dot_general | solution.py:21
  350.1 5.3 all-gather.12.cloned.1.call-done
  355.4 159.7 %multiply_convert_fusion = (bf16[4096,8960]{1,0:T(8,128)(2,1)}, f32[4096,8960]{1,0:T(8,128)}) fusion(f32[4096,8960]{1,0:T(8,128)} %fusion.35, bf16[4096,1536]{1,0:T(8,128)(2,1)} %fusion.20, bf16[1536,8960]{1,0:T(8,128)(2,1)} %all-gather.12.cloned.1.call-done), kind=kOutput, calls=%fused_computation.7 | convolution fusion | flops 112963092480 | bytes 407109632 | tf_op jit(solution)/shard_map/td,df->tf/dot_general | solution.py:21
  515.1 127.7 %fusion.36 = f32[8960,1536]{1,0:T(8,128)} fusion(bf16[4096,8960]{1,0:T(8,128)(2,1)} %get-tuple-element.39, bf16[4096,1536]{1,0:T(8,128)(2,1)} %bitcast.57), kind=kOutput, calls=%fused_computation.70 | convolution fusion | flops 112742891520 | bytes 141033472 | tf_op jit(solution)/shard_map/tf,td->fd/dot_general | solution.py:21
  642.8 182.0 %fusion.4 = (bf16[4096,8960]{1,0:T(8,128)(2,1)}, bf16[4096,8960]{1,0:T(8,128)(2,1)}) fusion(f32[4096,8960]{1,0:T(8,128)} %fusion.35, f32[4096,8960]{1,0:T(8,128)} %get-tuple-element.67, bf16[4096,1536]{1,0:T(8,128)(2,1)} %bitcast.58, bf16[8960,1536]{1,0:T(8,128)(2,1)} %all-gather.14.cloned.1.call-done), kind=kOutput, calls=%fused_computation.6 | convolution fusion | flops 113293393920 | bytes 480509952 | tf_op jit(solution)/shard_map/td,fd->tf/dot_general | solution.py:21
  824.8 129.0 %fusion.37 = f32[1536,8960]{1,0:T(8,128)} fusion(bf16[4096,1536]{1,0:T(8,128)(2,1)} %fusion.20, bf16[4096,8960]{1,0:T(8,128)(2,1)} %get-tuple-element.34), kind=kOutput, calls=%fused_computation.71 | convolution fusion | flops 112742891520 | bytes 141033472 | tf_op jit(solution)/shard_map/td,tf->df/dot_general | solution.py:21
  953.8 129.6 %fusion.38 = f32[1536,8960]{1,0:T(8,128)} fusion(bf16[4096,1536]{1,0:T(8,128)(2,1)} %fusion.20, bf16[4096,8960]{1,0:T(8,128)(2,1)} %get-tuple-element.35), kind=kOutput, calls=%fused_computation.72 | convolution fusion | flops 112742891520 | bytes 141033472 | tf_op jit(solution)/shard_map/td,tf->df/dot_general | solution.py:21
  1083.3 125.3 %fusion.39 = f32[4096,1536]{1,0:T(8,128)} fusion(bf16[4096,8960]{1,0:T(8,128)(2,1)} %get-tuple-element.34, bf16[1536,8960]{1,0:T(8,128)(2,1)} %all-gather.10.cloned.1.call-done), kind=kOutput, calls=%fused_computation.73 | convolution fusion | flops 112742891520 | bytes 126091264 | tf_op jit(solution)/shard_map/tf,df->td/dot_general | solution.py:21
  1208.6 135.9 %fusion.22 = (f32[1536]{0:T(1024)}, f32[4096]{0:T(1024)S(1)}, bf16[4096,1536]{1,0:T(8,128)(2,1)}) fusion(bf16[4096,1536]{1,0:T(8,128)(2,1)} %get-tuple-element.65, f32[4096]{0:T(1024)S(1)} %copy-done.7, f32[1536]{0:T(1024)S(1)} %copy-done.11, f32[4096,1536]{1,0:T(8,128)} %fusion.39, bf16[4096,8960]{1,0:T(8,128)(2,1)} %get-tuple-element.35, ...), kind=kOutput, calls=%fused_computation.33 | convolution fusion | flops 112805806080 | bytes 151302144 | tf_op jit(solution)/shard_map/tf,df->td/dot_general | solution.py:21
  1344.6 14.9 fusion.18
  1359.4 4.5 copy-done.2
  1364.0 24.5 fusion.40
  1388.4 26.1 convolution_convert_fusion.1.do_ref
  1414.5 88.7 %attn_bwd.1 = (bf16[4096,2048]{1,0:T(8,128)(2,1)}, f32[8,1,2048]{2,1,0:T(1,128)S(1)}) custom-call(bf16[4096,1536]{1,0:T(8,128)(2,1)} %get-tuple-element.29.q_ref, bf16[4096,256]{1,0:T(8,128)(2,1)S(1)} %get-tuple-element.30.k_ref, bf16[4096,256]{1,0:T(8,128)(2,1)S(1)} %copy-done.1, bf16[4096,1536]{1,0:T(8,128)(2,1)} %convolution_convert_fusion.1.do_ref, ...), custom_call_target="tpu_custom_call" | custom-call | flops 72477573120 | bytes 50331648 | tf_op jit(solution)/shard_map/attn_bwd/pallas_call | solution.py:178
  1503.2 34.6 %fusion.41 = f32[1536,2048]{1,0:T(8,128)} fusion(bf16[4096,1536]{1,0:T(8,128)(2,1)} %copy-done.3, bf16[4096,2048]{1,0:T(8,128)(2,1)} %get-tuple-element.40), kind=kOutput, calls=%fused_computation.75 | convolution fusion | flops 25769803776 | bytes 41943040 | tf_op jit(solution)/shard_map/td,te->de/dot_general | solution.py:21
  1540.8 37.2 %fusion.19 = (f32[1536]{0:T(1024)S(1)}, f32[4096]{0:T(1024)S(1)}, bf16[4096,1536]{1,0:T(8,128)(2,1)}) fusion(bf16[8,512,1536]{2,1,0:T(8,128)(2,1)} %param.15, f32[4096]{0:T(1024)S(1)} %bitcast.64, f32[1536]{0:T(1024)S(1)} %copy-done.9, bf16[4096,2048]{1,0:T(8,128)(2,1)} %get-tuple-element.40, bf16[1536,2176]{1,0:T(8,128)(2,1)} %all-gather.6.cloned.1.call-done), kind=kOutput, calls=%fused_computation.30 | convolution fusion | flops 25826420736 | bytes 48279552 | tf_op jit(solution)/shard_map/te,de->td/dot_general | solution.py:21
  1578.0 23.6 all-reduce.7
  1604.7 19.3 fusion.15
  1624.0 131.8 %fusion.24 = bf16[4096,1536]{1,0:T(8,128)(2,1)} fusion(bf16[4096,1536]{1,0:T(8,128)(2,1)} %get-tuple-element.65, bf16[4096,8960]{1,0:T(8,128)(2,1)} %get-tuple-element.39, bf16[8960,1536]{1,0:T(8,128)(2,1)} %all-gather.14.cloned.1.call-done), kind=kOutput, calls=%fused_computation.35 | convolution fusion | flops 112761765888 | bytes 126091264 | tf_op jit(solution)/shard_map/tf,fd->td/dot_general | solution.py:21
  1760.4 244.6 %reduce-scatter.12.cloned.1.call-done = f32[192,8960]{1,0:T(8,128)} async-done(((f32[1536,8960]{1,0:T(8,128)}), f32[192,8960]{1,0:T(8,128)}) %reduce-scatter.12.cloned.1.call-update) | async-done | bytes 6881296 | tf_op jit(solution)/shard_map/reduce_scatter | solution.py:227
  2004.9 309.7 %reduce-scatter.10.cloned.1.call-done = f32[192,8960]{1,0:T(8,128)} async-done(((f32[1536,8960]{1,0:T(8,128)}), f32[192,8960]{1,0:T(8,128)}) %reduce-scatter.10.cloned.1.call-update) | async-done | bytes 6881296 | tf_op jit(solution)/shard_map/reduce_scatter | solution.py:227
  2314.6 309.5 %reduce-scatter.14.cloned.1.call-done = f32[1120,1536]{1,0:T(8,128)} async-done(((f32[8960,1536]{1,0:T(8,128)}), f32[1120,1536]{1,0:T(8,128)}) %reduce-scatter.14.cloned.1.call-update) | async-done | bytes 6881296 | tf_op jit(solution)/shard_map/reduce_scatter | solution.py:227
  (89 shorter events, 25.1 us)
Async XLA Ops:
  7.2 16.0 copy-start.12
  7.2 50.3 %all-gather.6.cloned.1.call-start = ((), (), s32[]{:S(2)}) async-start(), calls=%async_computation.5 | async-start | bytes 7520256 | tf_op jit(solution)/shard_map/all_gather | solution.py:223
  13.1 155.5 %all-gather.8.cloned.1.call-start = ((), (), s32[]{:S(2)}) async-start(), calls=%async_computation.6 | async-start | bytes 5308416 | tf_op jit(solution)/shard_map/all_gather | solution.py:223
  13.8 210.3 %all-gather.10.cloned.1.call-start = ((), (), s32[]{:S(2)}) async-start(), calls=%async_computation.7 | async-start | bytes 30965760 | tf_op jit(solution)/shard_map/all_gather | solution.py:223
  14.6 340.8 %all-gather.12.cloned.1.call-start = ((), (), s32[]{:S(2)}) async-start(), calls=%async_computation.8 | async-start | bytes 30965760 | tf_op jit(solution)/shard_map/all_gather | solution.py:223
  15.1 627.7 %all-gather.14.cloned.1.call-start = ((), (), s32[]{:S(2)}) async-start(), calls=%async_computation.9 | async-start | bytes 30965760 | tf_op jit(solution)/shard_map/all_gather | solution.py:223
  15.7 1740.1 %reduce-scatter.6.cloned.1.call-start = ((), (), s32[]{:S(2)}) async-start(), calls=%async_computation.10 | async-start | bytes 14155776 | tf_op jit(solution)/shard_map/reduce_scatter | solution.py:227
  23.2 78.8 %copy-start.4 = (f32[1,4,8,128]{3,1,2,0:T(4,128)}, f32[1,4,8,128]{3,1,2,0:T(4,128)S(1)}, u32[]{:S(2)}) copy-start(f32[1,4,8,128]{3,1,2,0:T(4,128)S(1)} %copy.45) | copy-start | bytes 49156
  57.5 11.9 slice-start
  60.7 0.6 copy-start.8
  60.7 138.3 %copy-start.10 = (f32[1536]{0:T(1024)}, f32[1536]{0:T(1024)S(1)}, u32[]{:S(2)}) copy-start(f32[1536]{0:T(1024)S(1)} %get-tuple-element.46) | copy-start | bytes 18436
  61.3 8.1 slice-start.1
  69.4 32.5 %copy-start.3 = (bf16[4096,1536]{1,0:T(8,128)(2,1)}, bf16[4096,1536]{1,0:T(8,128)(2,1)S(1)}, u32[]{:S(2)}) copy-start(bf16[4096,1536]{1,0:T(8,128)(2,1)S(1)} %fusion.27) | copy-start | bytes 37748740
  167.3 1.3 copy-start
  199.0 0.6 copy-start.6
  1083.3 125.3 %copy-start.7 = (f32[4096]{0:T(1024)S(1)}, f32[4096]{0:T(1024)}, u32[]{:S(2)}) copy-start(f32[4096]{0:T(1024)} %copy-done.6) | copy-start | bytes 49156
  1083.3 125.3 %copy-start.11 = (f32[1536]{0:T(1024)S(1)}, f32[1536]{0:T(1024)}, u32[]{:S(2)}) copy-start(f32[1536]{0:T(1024)} %copy-done.10) | copy-start | bytes 18436
  1359.4 4.5 copy-start.2
  1388.4 26.1 copy-start.1
  1537.8 222.5 %reduce-scatter.8.cloned.1.call-start = ((), (), s32[]{:S(2)}) async-start(), calls=%async_computation.11 | async-start | bytes 10616832 | tf_op jit(solution)/shard_map/reduce_scatter | solution.py:227
  1538.6 466.4 %reduce-scatter.12.cloned.1.call-start = ((), (), s32[]{:S(2)}) async-start(), calls=%async_computation.13 | async-start | bytes 61931520 | tf_op jit(solution)/shard_map/reduce_scatter | solution.py:227
  1539.3 775.3 %reduce-scatter.10.cloned.1.call-start = ((), (), s32[]{:S(2)}) async-start(), calls=%async_computation.12 | async-start | bytes 61931520 | tf_op jit(solution)/shard_map/reduce_scatter | solution.py:227
  1540.1 0.7 copy-start.5
  1540.1 0.7 copy-start.9
  1540.1 1084.1 %reduce-scatter.14.cloned.1.call-start = ((), (), s32[]{:S(2)}) async-start(), calls=%async_computation.14 | async-start | bytes 61931520 | tf_op jit(solution)/shard_map/reduce_scatter | solution.py:227
  1540.8 37.2 %copy-start.13 = (f32[1536]{0:T(1024)S(1)}, f32[1536]{0:T(1024)}, u32[]{:S(2)}) copy-start(f32[1536]{0:T(1024)} %get-tuple-element.42) | copy-start | bytes 18436
Sparse Core Ops, SparseCore 0:
  13.2 44.2 all-gather.5
  59.3 33.2 all-gather.7
  94.4 129.6 all-gather.9
  225.7 129.5 all-gather.11
  357.0 129.5 all-gather.13
  1537.9 84.7 reduce-scatter.5
  1626.7 68.4 reduce-scatter.7
  1699.4 305.5 reduce-scatter.11
  2009.1 305.5 reduce-scatter.9
  2318.6 305.5 reduce-scatter.13

commit v2 on v1

--- a/solution.py
+++ b/solution.py
@@ -305,9 +305,17 @@
         layer_out = (resid_mid.astype(jnp.float32) + matmul_f32('tf,fd->td', act_last, w_down)).astype(jnp.bfloat16)
 
         d_bias = jnp.sum(d_bias_rows, axis=(0, 1))
-        g_gain_attn, g_gain_mlp = scatter_rows(d_gain_attn), scatter_rows(d_gain_mlp)
-        g_bq = scatter_rows(d_bias[:n_q])
-        g_bk, g_bv = scatter_rows(d_bias[n_q:n_q + n_kv_w]), scatter_rows(d_bias[n_q + n_kv_w:])
+        kv_shard = n_kv_w // n_dev
+
+        def kv_column(vec):
+            return jnp.pad(vec.reshape(n_dev, kv_shard), ((0, 0), (0, n_rows - kv_shard))).reshape(n_model)
+
+        vec_rows = jnp.stack([d_gain_attn, d_gain_mlp, d_bias[:n_q], kv_column(d_bias[n_q:n_q + n_kv_w]), kv_column(d_bias[n_q + n_kv_w:])])
+        vec_rows = jnp.pad(vec_rows, ((0, 3), (0, 0))).reshape(8, n_dev, n_rows).transpose(1, 0, 2)
+        vec_rows = jnp.pad(vec_rows, ((0, 0), (0, 0), (0, 256 - n_rows))).reshape(n_dev * 8, 256)
+        g_vecs = scatter_rows(vec_rows)
+        g_gain_attn, g_gain_mlp, g_bq = g_vecs[0, :n_rows], g_vecs[1, :n_rows], g_vecs[2, :n_rows]
+        g_bk, g_bv = g_vecs[3, :kv_shard], g_vecs[4, :kv_shard]
         g_wq, g_wk, g_wv = g_qkv[:, :n_q], g_qkv[:, n_q:n_q + n_kv_w], g_qkv[:, n_q + n_kv_w:]
         return (layer_out.reshape(hidden3.shape), grad_hidden.reshape(hidden3.shape), g_gain_attn, g_wq, g_bq, g_wk, g_bk, g_wv, g_bv, g_o, g_gain_mlp, g_gate, g_up, g_down)
 

time: 2640 us -> 2700 us (1.023)
  waiting for transfers between devices: 911 us -> 1000 us
    reduce_scatter x5 -> x6, waiting for transfers between devices: 864 us -> 954 us  [scatter_rows(): lax.psum_scatter(grad_part, FSDP_AXIS, scatter_dimension=0, tiled=True)]
  transfers between devices with their start and end apart: 10 -> 11, of which waited for: 6 -> 7; matrix products, arithmetic and copies ran while one was open for 27% -> 25% of each run, Pallas kernels for 2% -> 2%
where the time goes in v2:
time: 2700 us; the launch traced here: 2690 us
  matrix products  1430 us (53%)
  waiting for transfers between devices  1000 us (37%)
  Pallas kernels  154 us (6%)
  other arithmetic  74.8 us (3%)
    dot_general x15, matrix products, matmul_f32(): jnp.einsum(eq_form, lhs_arr, rhs_arr, preferred_element_type=jnp.float32)  1430 us
    reduce_scatter x6, waiting for transfers between devices, scatter_rows(): lax.psum_scatter(grad_part, FSDP_AXIS, scatter_dimension=0, tiled=True)  954 us
    pallas_call x1, Pallas kernels, attention_bwd(): pl.pallas_call(functools.partial(attn_bwd_kernel, n_group, n_q, n_kv_w),...  88.8 us
    pallas_call x1, Pallas kernels, attention_fwd(): pl.pallas_call(functools.partial(attn_fwd_kernel, n_group), grid=(n_batch...  65.4 us
  transfers between devices with their start and end apart: 11, of which 7 were waited for; matrix products, arithmetic and copies ran while one was open for 25% of the time, Pallas kernels for 2%

profile of v2, /device:TPU:0, one launch (start us, length us, event | category | flops | bytes accessed | tf_op | source)
XLA Modules:
  0.0 2694.6 jit_solution(8754063050373614565)
XLA Ops:
  16.5 7.6 fusion.28
  24.1 7.5 fusion.32
  31.6 3.2 pad_maximum_fusion
  34.8 22.7 all-gather.6.cloned.1.call-done
  61.3 8.1 fusion.27
  69.7 31.9 %convolution_add_fusion.q_ref.k_ref.v_ref = f32[4096,2048]{1,0:T(8,128)} fusion(bf16[4096,1536]{1,0:T(8,128)(2,1)S(1)} %fusion.27, f32[2048]{0:T(1024)S(1)} %maximum_convert_fusion, bf16[1536,2176]{1,0:T(8,128)(2,1)S(1)} %bitcast.72), kind=kOutput, calls=%fused_computation.45 | convolution fusion | flops 25778192384 | bytes 52436992 | tf_op jit(solution)/shard_map/td,de->te/dot_general | solution.py:21
  101.7 65.4 %attn_fwd.1 = (bf16[4096,1536]{1,0:T(8,128)(2,1)}, bf16[4096,1536]{1,0:T(8,128)(2,1)}, bf16[4096,256]{1,0:T(8,128)(2,1)S(1)}, bf16[4096,256]{1,0:T(8,128)(2,1)S(1)}, f32[16,8,512]{2,1,0:T(8,128)S(1)}) custom-call(f32[4096,2048]{1,0:T(8,128)} %convolution_add_fusion.q_ref.k_ref.v_ref, f32[4096,2048]{1,0:T(8,128)} %convolution_add_fusion.q_ref.k_ref.v_ref, ...), custom_call_target="tpu_custom_call" | custom-call | flops 28991029248 | bytes 62914560 | tf_op jit(solution)/shard_map/attn_fwd/pallas_call | solution.py:141
  168.4 30.7 %fusion.23 = (f32[4096]{0:T(1024)S(1)}, bf16[4096,1536]{1,0:T(8,128)(2,1)}) fusion(bf16[4096,1536]{1,0:T(8,128)(2,1)} %get-tuple-element.28, bf16[1536,1536]{1,0:T(8,128)(2,1)} %all-gather.8.cloned.1.call-done, bf16[8,512,1536]{2,1,0:T(8,128)(2,1)} %param.15), kind=kOutput, calls=%fused_computation.34 | convolution fusion | flops 19365097472 | bytes 42483712 | tf_op jit(solution)/shard_map/te,ed->td/dot_general | solution.py:21
  199.8 11.8 fusion.20
  211.6 12.5 all-gather.10.cloned.1.call-done
  224.0 126.1 %fusion.36 = f32[4096,8960]{1,0:T(8,128)} fusion(bf16[4096,1536]{1,0:T(8,128)(2,1)} %fusion.20, bf16[1536,8960]{1,0:T(8,128)(2,1)} %all-gather.10.cloned.1.call-done), kind=kOutput, calls=%fused_computation.73 | convolution fusion | flops 112742891520 | bytes 186908672 | tf_op jit(solution)/shard_map/td,df->tf/dot_general | solution.py:21
  350.1 5.2 all-gather.12.cloned.1.call-done
  355.3 159.5 %multiply_convert_fusion = (bf16[4096,8960]{1,0:T(8,128)(2,1)}, f32[4096,8960]{1,0:T(8,128)}) fusion(f32[4096,8960]{1,0:T(8,128)} %fusion.36, bf16[4096,1536]{1,0:T(8,128)(2,1)} %fusion.20, bf16[1536,8960]{1,0:T(8,128)(2,1)} %all-gather.12.cloned.1.call-done), kind=kOutput, calls=%fused_computation.7 | convolution fusion | flops 112963092480 | bytes 407109632 | tf_op jit(solution)/shard_map/td,df->tf/dot_general | solution.py:21
  514.8 127.4 %fusion.37 = f32[8960,1536]{1,0:T(8,128)} fusion(bf16[4096,8960]{1,0:T(8,128)(2,1)} %get-tuple-element.39, bf16[4096,1536]{1,0:T(8,128)(2,1)} %bitcast.67), kind=kOutput, calls=%fused_computation.74 | convolution fusion | flops 112742891520 | bytes 141033472 | tf_op jit(solution)/shard_map/tf,td->fd/dot_general | solution.py:21
  642.2 181.9 %fusion.4 = (bf16[4096,8960]{1,0:T(8,128)(2,1)}, bf16[4096,8960]{1,0:T(8,128)(2,1)}) fusion(f32[4096,8960]{1,0:T(8,128)} %fusion.36, f32[4096,8960]{1,0:T(8,128)} %get-tuple-element.67, bf16[4096,1536]{1,0:T(8,128)(2,1)} %bitcast.68, bf16[8960,1536]{1,0:T(8,128)(2,1)} %all-gather.14.cloned.1.call-done), kind=kOutput, calls=%fused_computation.6 | convolution fusion | flops 113293393920 | bytes 480509952 | tf_op jit(solution)/shard_map/td,fd->tf/dot_general | solution.py:21
  824.1 128.9 %fusion.38 = f32[1536,8960]{1,0:T(8,128)} fusion(bf16[4096,1536]{1,0:T(8,128)(2,1)} %fusion.20, bf16[4096,8960]{1,0:T(8,128)(2,1)} %get-tuple-element.34), kind=kOutput, calls=%fused_computation.75 | convolution fusion | flops 112742891520 | bytes 141033472 | tf_op jit(solution)/shard_map/td,tf->df/dot_general | solution.py:21
  953.1 129.7 %fusion.39 = f32[1536,8960]{1,0:T(8,128)} fusion(bf16[4096,1536]{1,0:T(8,128)(2,1)} %fusion.20, bf16[4096,8960]{1,0:T(8,128)(2,1)} %get-tuple-element.35), kind=kOutput, calls=%fused_computation.76 | convolution fusion | flops 112742891520 | bytes 141033472 | tf_op jit(solution)/shard_map/td,tf->df/dot_general | solution.py:21
  1082.8 125.2 %fusion.40 = f32[4096,1536]{1,0:T(8,128)} fusion(bf16[4096,8960]{1,0:T(8,128)(2,1)} %get-tuple-element.34, bf16[1536,8960]{1,0:T(8,128)(2,1)} %all-gather.10.cloned.1.call-done), kind=kOutput, calls=%fused_computation.77 | convolution fusion | flops 112742891520 | bytes 126091264 | tf_op jit(solution)/shard_map/tf,df->td/dot_general | solution.py:21
  1208.1 135.4 %fusion.22 = (f32[1536]{0:T(1024)S(1)}, f32[4096]{0:T(1024)S(1)}, bf16[4096,1536]{1,0:T(8,128)(2,1)}) fusion(bf16[4096,1536]{1,0:T(8,128)(2,1)} %get-tuple-element.65, f32[4096]{0:T(1024)S(1)} %copy-done.7, f32[1536]{0:T(1024)S(1)} %copy-done.11, f32[4096,1536]{1,0:T(8,128)} %fusion.40, bf16[4096,8960]{1,0:T(8,128)(2,1)} %get-tuple-element.35, ...), kind=kOutput, calls=%fused_computation.33 | convolution fusion | flops 112805806080 | bytes 151302144 | tf_op jit(solution)/shard_map/tf,df->td/dot_general | solution.py:21
  1344.0 14.9 fusion.18
  1358.9 4.6 copy-done.2
  1363.5 24.3 fusion.41
  1387.8 26.1 convolution_convert_fusion.1.do_ref
  1413.9 88.8 %attn_bwd.1 = (bf16[4096,2048]{1,0:T(8,128)(2,1)}, f32[8,1,2048]{2,1,0:T(1,128)S(1)}) custom-call(bf16[4096,1536]{1,0:T(8,128)(2,1)} %get-tuple-element.29.q_ref, bf16[4096,256]{1,0:T(8,128)(2,1)S(1)} %get-tuple-element.30.k_ref, bf16[4096,256]{1,0:T(8,128)(2,1)S(1)} %copy-done.1, bf16[4096,1536]{1,0:T(8,128)(2,1)} %convolution_convert_fusion.1.do_ref, ...), custom_call_target="tpu_custom_call" | custom-call | flops 72477573120 | bytes 50331648 | tf_op jit(solution)/shard_map/attn_bwd/pallas_call | solution.py:178
  1502.7 34.6 %fusion.42 = f32[1536,2048]{1,0:T(8,128)} fusion(bf16[4096,1536]{1,0:T(8,128)(2,1)} %copy-done.3, bf16[4096,2048]{1,0:T(8,128)(2,1)} %get-tuple-element.40), kind=kOutput, calls=%fused_computation.79 | convolution fusion | flops 25769803776 | bytes 41943040 | tf_op jit(solution)/shard_map/td,te->de/dot_general | solution.py:21
  1537.8 35.3 %fusion.19 = (f32[1536]{0:T(1024)S(1)}, f32[4096]{0:T(1024)S(1)}, bf16[4096,1536]{1,0:T(8,128)(2,1)}) fusion(bf16[8,512,1536]{2,1,0:T(8,128)(2,1)} %param.15, f32[4096]{0:T(1024)S(1)} %bitcast.75, f32[1536]{0:T(1024)S(1)} %copy-done.9, bf16[4096,2048]{1,0:T(8,128)(2,1)} %get-tuple-element.40, bf16[1536,2176]{1,0:T(8,128)(2,1)} %all-gather.6.cloned.1.call-done), kind=kOutput, calls=%fused_computation.30 | convolution fusion | flops 25826420736 | bytes 48279552 | tf_op jit(solution)/shard_map/te,de->td/dot_general | solution.py:21
  1577.5 19.4 fusion.15
  1596.9 130.1 %fusion.24 = bf16[4096,1536]{1,0:T(8,128)(2,1)} fusion(bf16[4096,1536]{1,0:T(8,128)(2,1)} %get-tuple-element.65, bf16[4096,8960]{1,0:T(8,128)(2,1)} %get-tuple-element.39, bf16[8960,1536]{1,0:T(8,128)(2,1)} %all-gather.14.cloned.1.call-done), kind=kOutput, calls=%fused_computation.35 | convolution fusion | flops 112761765888 | bytes 126091264 | tf_op jit(solution)/shard_map/tf,fd->td/dot_general | solution.py:21
  1733.8 25.2 reduce-scatter.11.cloned.1.call-done
  1759.0 309.7 %reduce-scatter.17.cloned.1.call-done = f32[1120,1536]{1,0:T(8,128)} async-done(((f32[8960,1536]{1,0:T(8,128)}), f32[1120,1536]{1,0:T(8,128)}) %reduce-scatter.17.cloned.1.call-update) | async-done | bytes 6881296 | tf_op jit(solution)/shard_map/reduce_scatter | solution.py:227
  2068.7 309.5 %reduce-scatter.13.cloned.1.call-done = f32[192,8960]{1,0:T(8,128)} async-done(((f32[1536,8960]{1,0:T(8,128)}), f32[192,8960]{1,0:T(8,128)}) %reduce-scatter.13.cloned.1.call-update) | async-done | bytes 6881296 | tf_op jit(solution)/shard_map/reduce_scatter | solution.py:227
  2378.2 309.7 %reduce-scatter.15.cloned.1.call-done = f32[192,8960]{1,0:T(8,128)} async-done(((f32[1536,8960]{1,0:T(8,128)}), f32[192,8960]{1,0:T(8,128)}) %reduce-scatter.15.cloned.1.call-update) | async-done | bytes 6881296 | tf_op jit(solution)/shard_map/reduce_scatter | solution.py:227
  (100 shorter events, 27.4 us)
Async XLA Ops:
  7.2 50.3 %all-gather.6.cloned.1.call-start = ((), (), s32[]{:S(2)}) async-start(), calls=%async_computation.6 | async-start | bytes 7520256 | tf_op jit(solution)/shard_map/all_gather | solution.py:223
  13.0 155.4 %all-gather.8.cloned.1.call-start = ((), (), s32[]{:S(2)}) async-start(), calls=%async_computation.7 | async-start | bytes 5308416 | tf_op jit(solution)/shard_map/all_gather | solution.py:223
  13.8 210.2 %all-gather.10.cloned.1.call-start = ((), (), s32[]{:S(2)}) async-start(), calls=%async_computation.8 | async-start | bytes 30965760 | tf_op jit(solution)/shard_map/all_gather | solution.py:223
  14.5 340.8 %all-gather.12.cloned.1.call-start = ((), (), s32[]{:S(2)}) async-start(), calls=%async_computation.9 | async-start | bytes 30965760 | tf_op jit(solution)/shard_map/all_gather | solution.py:223
  15.1 627.1 %all-gather.14.cloned.1.call-start = ((), (), s32[]{:S(2)}) async-start(), calls=%async_computation.10 | async-start | bytes 30965760 | tf_op jit(solution)/shard_map/all_gather | solution.py:223
  15.7 1711.2 %reduce-scatter.7.cloned.1.call-start = ((), (), s32[]{:S(2)}) async-start(), calls=%async_computation.11 | async-start | bytes 73728 | tf_op jit(solution)/shard_map/reduce_scatter | solution.py:227
  24.1 77.6 %copy-start.4 = (f32[1,4,8,128]{3,1,2,0:T(4,128)}, f32[1,4,8,128]{3,1,2,0:T(4,128)S(1)}, u32[]{:S(2)}) copy-start(f32[1,4,8,128]{3,1,2,0:T(4,128)S(1)} %copy.47) | copy-start | bytes 49156
  57.5 11.9 slice-start
  60.7 0.6 copy-start.8
  60.7 138.5 %copy-start.10 = (f32[1536]{0:T(1024)}, f32[1536]{0:T(1024)S(1)}, u32[]{:S(2)}) copy-start(f32[1536]{0:T(1024)S(1)} %get-tuple-element.46) | copy-start | bytes 18436
  61.3 8.1 slice-start.1
  69.4 32.3 %copy-start.3 = (bf16[4096,1536]{1,0:T(8,128)(2,1)}, bf16[4096,1536]{1,0:T(8,128)(2,1)S(1)}, u32[]{:S(2)}) copy-start(bf16[4096,1536]{1,0:T(8,128)(2,1)S(1)} %fusion.27) | copy-start | bytes 37748740
  167.1 1.3 copy-start
  199.2 0.6 copy-start.6
  1082.8 125.3 %copy-start.7 = (f32[4096]{0:T(1024)S(1)}, f32[4096]{0:T(1024)}, u32[]{:S(2)}) copy-start(f32[4096]{0:T(1024)} %copy-done.6) | copy-start | bytes 49156
  1082.8 125.3 %copy-start.11 = (f32[1536]{0:T(1024)S(1)}, f32[1536]{0:T(1024)}, u32[]{:S(2)}) copy-start(f32[1536]{0:T(1024)} %copy-done.10) | copy-start | bytes 18436
  1358.9 4.6 copy-start.2
  1387.8 26.1 copy-start.1
  1502.7 35.0 %copy-start.5 = (f32[1,4,8,128]{3,1,2,0:T(4,128)S(1)}, f32[1,4,8,128]{3,1,2,0:T(4,128)}, u32[]{:S(2)}) copy-start(f32[1,4,8,128]{3,1,2,0:T(4,128)} %copy-done.4) | copy-start | bytes 49156
  1502.7 35.0 %copy-start.9 = (f32[1536]{0:T(1024)S(1)}, f32[1536]{0:T(1024)}, u32[]{:S(2)}) copy-start(f32[1536]{0:T(1024)} %copy-done.8) | copy-start | bytes 18436
  1537.7 35.4 %copy-start.12 = (f32[1,1536]{1,0:T(1,128)S(1)}, f32[1,1536]{1,0:T(1,128)}, u32[]{:S(2)}) copy-start(f32[1,1536]{1,0:T(1,128)} %stack.13) | copy-start | bytes 18436
  1574.0 155.6 %reduce-scatter.9.cloned.1.call-start = ((), (), s32[]{:S(2)}) async-start(), calls=%async_computation.12 | async-start | bytes 14155776 | tf_op jit(solution)/shard_map/reduce_scatter | solution.py:227
  1574.7 184.3 %reduce-scatter.11.cloned.1.call-start = ((), (), s32[]{:S(2)}) async-start(), calls=%async_computation.13 | async-start | bytes 10616832 | tf_op jit(solution)/shard_map/reduce_scatter | solution.py:227
  1575.5 493.2 %reduce-scatter.17.cloned.1.call-start = ((), (), s32[]{:S(2)}) async-start(), calls=%async_computation.16 | async-start | bytes 61931520 | tf_op jit(solution)/shard_map/reduce_scatter | solution.py:227
  1576.2 802.0 %reduce-scatter.13.cloned.1.call-start = ((), (), s32[]{:S(2)}) async-start(), calls=%async_computation.14 | async-start | bytes 61931520 | tf_op jit(solution)/shard_map/reduce_scatter | solution.py:227
  1576.8 1111.1 %reduce-scatter.15.cloned.1.call-start = ((), (), s32[]{:S(2)}) async-start(), calls=%async_computation.15 | async-start | bytes 61931520 | tf_op jit(solution)/shard_map/reduce_scatter | solution.py:227
Sparse Core Ops, SparseCore 0:
  13.2 44.2 all-gather.5
  59.3 33.2 all-gather.7
  94.4 129.5 all-gather.9
  225.7 129.5 all-gather.11
  357.0 129.6 all-gather.13
  1574.1 24.9 reduce-scatter.6
  1602.5 83.9 reduce-scatter.8
  1690.5 68.4 reduce-scatter.10
  1763.1 305.5 reduce-scatter.16
  2072.6 305.5 reduce-scatter.12
  2382.3 305.5 reduce-scatter.14
